TPU v7x, 256 devices: a whole 4x4x8 slice. The times are simulated.
256 devices in a mesh: ens: 4 (over x), batch: 16 (over z, core), cols: 4 (over y).
Axes of the slice: x: 4, y: 4, z: 8, core: 2. Of those that a mesh axis runs over, the one named last changes fastest.
Arguments:
- grad_up: bfloat16 [64, 1280, 5120], P(('ens', 'batch'), None, 'cols'), parts along dimension 0, may hold values from -0.875 to 0.875
- grad_down: bfloat16 [64, 5120, 1280], P(('ens', 'batch'), 'cols'), parts along dimension 0, may hold values from -0.875 to 0.875
- grad_norm: bfloat16 [64, 1280], P(('ens', 'batch')), parts along dimension 0, may hold values from -8 to 8
- grad_bias: bfloat16 [64, 1280], P(('ens', 'batch')), parts along dimension 0, may hold values from -8 to 8
- weight_up: float32 [5120, 5120], P(('ens', 'batch'), 'cols'), parts along dimension 0, may hold values from -0.25 to 0.25
- weight_down: float32 [20480, 1280], P(('ens', 'cols'), 'batch'), parts along dimension 0, may hold values from -0.125 to 0.125
- weight_norm: float32 [5120], P(('ens', 'batch')), parts along dimension 0, may hold values from 0.25 to 1.75
- weight_bias: float32 [5120], P(('ens', 'batch')), parts along dimension 0, may hold values from -3 to 3
Outputs:
- copy_up: bfloat16 [5120, 5120], P('ens', 'cols'), parts along dimension 0
- copy_down: bfloat16 [20480, 1280], P(('ens', 'cols')), parts along dimension 0
- copy_norm: bfloat16 [5120], P('ens'), parts along dimension 0
- copy_bias: bfloat16 [5120], P('ens'), parts along dimension 0
- new_up: float32 [5120, 5120], P(('ens', 'batch'), 'cols'), parts along dimension 0
- new_down: float32 [20480, 1280], P(('ens', 'cols'), 'batch'), parts along dimension 0
- new_norm: float32 [5120], P(('ens', 'batch')), parts along dimension 0
- new_bias: float32 [5120], P(('ens', 'batch')), parts along dimension 0
There are 4 independent parts, one for each index of `ens`. A program takes and returns all parts, laid end to end along the dimension named above; each array names one. Nothing has to cross between parts.
All inputs are finite; a program needn't handle non-finite values.
Results may differ from a plain program's by a relative error of at most 0.014.
Values may be sent and summed in bfloat16 or wider, within the bound.
A program may use at most 128 MiB of HBM per device.

v0:
```python
import functools

import jax
import jax.numpy as jnp
from jax import lax
from jax.sharding import Mesh
from jax.sharding import PartitionSpec as P

BATCH = ("batch_0", "batch_1")
ENS_BATCH = ("ens", "batch_0", "batch_1")


learn_rate = 0.4


def split_up(array, dim, devices):
    before, after = (array.shape[:dim], array.shape[dim + 1 :])
    return jnp.moveaxis(array.reshape(*before, devices, -1, *after), dim, 0)


def sum_packed(arrays, axis, dims):
    devices = lax.axis_size(axis)
    parts = [split_up(a, dim, devices) for a, dim in zip(arrays, dims)]
    lines = jnp.concatenate([b.reshape(devices, -1) for b in parts], axis=1)
    rows = max(16, -(-lines.shape[1] // 1024) * 8)
    lines = jnp.pad(lines, ((0, 0), (0, rows * 128 - lines.shape[1]))).reshape(-1, 128)
    ravelled, at, gathered = (lax.psum_scatter(lines, axis, tiled=True).reshape(-1), 0, [])
    for b in parts:
        part = b[0]
        gathered.append(ravelled[at : at + part.size].reshape(part.shape))
        at += part.size
    return tuple(gathered)


def one_axis_at_a_time(array, axes):
    return functools.reduce(lax.psum, axes, array)


def copy_for_each(array, axis):
    copies = jnp.broadcast_to(array, (lax.axis_size(axis), *array.shape))
    return lax.all_to_all(copies, axis, split_axis=0, concat_axis=0, tiled=True)


def of_everyone(array, axis):
    everything = copy_for_each(array, axis)
    return jnp.sum(everything, axis=0)


def together(arrays, axis):
    ends = [0]
    for a in arrays:
        ends.append(ends[-1] + a.size)
    running = of_everyone(jnp.concatenate([a.ravel() for a in arrays]), axis)
    return tuple((running[b:e].reshape(a.shape) for a, b, e in zip(arrays, ends, ends[1:])))


def rows_first(arrays, axis, dims):
    turned = [jnp.moveaxis(a, dim, 0) for a, dim in zip(arrays, dims)]
    widths = [t[0].size for t in turned]
    both = jnp.concatenate([t.reshape(-1, w) for t, w in zip(turned, widths)], axis=1)
    out = lax.all_gather(both, axis, axis=0, tiled=True)
    parts = jnp.split(out, [sum(widths[:k]) for k in range(1, len(widths))], axis=1)
    return tuple(
        (
            jnp.moveaxis(b.reshape(-1, *t.shape[1:]), 0, dim)
            for b, t, dim in zip(parts, turned, dims)
        )
    )


def per_device(
    grad_up, grad_down, grad_norm, grad_bias, weight_up, weight_down, weight_norm, weight_bias
):
    mean_up, mean_down = tuple(
        (
            part.astype(jnp.float32)
            for part in sum_packed(
                (
                    grad_up[0].astype(jnp.float32).astype(jnp.bfloat16),
                    grad_down[0].astype(jnp.float32).astype(jnp.bfloat16),
                ),
                BATCH,
                (0, 1),
            )
        )
    )
    whole_norm, whole_bias = (
        one_axis_at_a_time(grad_norm[0].astype(jnp.float32), BATCH),
        one_axis_at_a_time(grad_bias[0].astype(jnp.float32), BATCH),
    )
    place = lax.axis_index(BATCH)
    mean_norm = lax.dynamic_slice_in_dim(
        whole_norm, place * weight_norm.shape[0], weight_norm.shape[0]
    )
    mean_bias = lax.dynamic_slice_in_dim(
        whole_bias, place * weight_bias.shape[0], weight_bias.shape[0]
    )
    mean_rate = lax.axis_size(BATCH) ** (-0.5)
    mean_up = mean_up * mean_rate
    mean_down = mean_down * mean_rate
    mean_norm = mean_norm * mean_rate
    mean_bias = mean_bias * mean_rate
    own_up, own_down, slope_up_norm, slope_down_norm = together(
        (
            jnp.sum(weight_up * weight_up, axis=1, keepdims=True),
            jnp.sum(weight_down * weight_down, axis=0, keepdims=True),
            jnp.sum(mean_up * mean_up, axis=1, keepdims=True),
            jnp.sum(mean_down * mean_down, axis=0, keepdims=True),
        ),
        "cols",
    )
    mean_up = mean_up * (jnp.sqrt(own_up) * lax.rsqrt(slope_up_norm + 1e-06))
    mean_down = mean_down * (jnp.sqrt(own_down) * lax.rsqrt(slope_down_norm + 1e-06))
    new_up = weight_up - learn_rate * mean_up
    new_down = weight_down - learn_rate * mean_down
    new_norm = weight_norm - learn_rate * mean_norm
    new_bias = weight_bias - learn_rate * mean_bias
    copy_up, copy_down, copy_norm, copy_bias = rows_first(
        (
            new_up.astype(jnp.bfloat16),
            new_down.astype(jnp.bfloat16),
            new_norm.astype(jnp.bfloat16),
            new_bias.astype(jnp.bfloat16),
        ),
        BATCH,
        (0, 1, 0, 0),
    )
    return (copy_up, copy_down, copy_norm, copy_bias, new_up, new_down, new_norm, new_bias)


def solution(mesh):
    finer = Mesh(
        mesh.devices.reshape(mesh.shape["ens"], 8, 2, mesh.shape["cols"]),
        ("ens", "batch_0", "batch_1", "cols"),
    )
    placed = (
        P(ENS_BATCH, None, "cols"),
        P(ENS_BATCH, "cols", None),
        P(ENS_BATCH, None),
        P(ENS_BATCH, None),
        P(ENS_BATCH, "cols"),
        P(("ens", "cols"), BATCH),
        P(ENS_BATCH),
        P(ENS_BATCH),
    )
    return jax.shard_map(
        per_device,
        mesh=finer,
        in_specs=placed,
        out_specs=(
            P("ens", "cols"),
            P(("ens", "cols"), None),
            P("ens"),
            P("ens"),
            P(ENS_BATCH, "cols"),
            P(("ens", "cols"), BATCH),
            P(ENS_BATCH),
            P(ENS_BATCH),
        ),
        check_vma=False,
    )
```

profile of v0, /device:TPU:1, one launch (start us, length us, event | category | flops | bytes accessed | tf_op | source)
XLA Modules:
  0.0 202.8 jit_solution(4405287460768067345)
XLA Ops:
  7.2 2.9 %reshape_reshape.3 = bf16[16,102400]{1,0:T(8,128)(2,1)S(1)} reshape(bf16[1,1280,1280]{2,1,0:T(8,128)(2,1)} %param.8) | data formatting | bytes 6553600 | tf_op jit(solution)/shard_map/reshape;reshape | solution.py:24
  10.2 5.7 %copy.38 = bf16[1,1280,1280]{1,2,0:T(8,128)(2,1)} copy(bf16[1,1280,1280]{2,1,0:T(8,128)(2,1)} %param.9) | data formatting | bytes 6553600 | tf_op args[1]
  15.8 7.3 %copy.39 = bf16[16,1280,80]{2,1,0:T(8,128)(2,1)} copy(bf16[16,1280,80]{1,2,0:T(8,128)(2,1)} %bitcast.11) | data formatting | bytes 6553600 | tf_op jit(solution)/shard_map/transpose | solution.py:18
  23.1 13.6 %reshape.74 = bf16[16,102400]{1,0:T(8,128)(2,1)} reshape(bf16[16,1280,80]{2,1,0:T(8,128)(2,1)} %copy.39) | data formatting | bytes 6553600 | tf_op jit(solution)/shard_map/reshape | solution.py:24
  36.7 8.6 %pad_maximum_fusion = bf16[16,204800]{1,0:T(8,128)(2,1)} fusion(bf16[16,102400]{1,0:T(8,128)(2,1)} %reshape.74, bf16[16,102400]{1,0:T(8,128)(2,1)S(1)} %reshape_reshape.3), kind=kLoop, calls=%fused_computation | loop fusion | flops 13107200 | bytes 13107200 | tf_op jit(solution)/shard_map/concatenate | solution.py:24
  45.3 6.6 %reshape.75 = bf16[25600,128]{1,0:T(8,128)(2,1)} reshape(bf16[16,204800]{1,0:T(8,128)(2,1)} %pad_maximum_fusion) | data formatting | bytes 13107200 | tf_op jit(solution)/shard_map/reshape | solution.py:26
  52.0 0.6 copy-done.2
  52.7 27.5 %all-reduce = (f32[1280]{0:T(1024)S(1)}, f32[1280]{0:T(1024)S(1)}) all-reduce(f32[1280]{0:T(1024)S(1)} %get-tuple-element.69, f32[1280]{0:T(1024)S(1)} %get-tuple-element.68), channel_id=1, replica_groups=mesh['ens'=4,'batch_0'=8,'batch_1'=2,'cols'=4] {'batch_0'}, use_global_device_ids=true, to_apply=%region_7.8 | all-reduce | flops 2560 | bytes 20480 | tf_op jit(solution)/shard_map/psum | solution.py:36
  80.1 9.9 %all-reduce.1 = (f32[1280]{0:T(1024)S(1)}, f32[1280]{0:T(1024)S(1)}) all-reduce(f32[1280]{0:T(1024)S(1)} %get-tuple-element.50, f32[1280]{0:T(1024)S(1)} %get-tuple-element.51), channel_id=1, replica_groups=mesh['ens'=4,'batch_0'=8,'batch_1'=2,'cols'=4] {'batch_1'}, use_global_device_ids=true, to_apply=%region_8.9 | all-reduce | flops 2560 | bytes 20480 | tf_op jit(solution)/shard_map/psum | solution.py:36
  90.3 0.6 convert_bitcast_fusion.2
  90.9 29.8 %reduce-scatter.2.cloned.1.call-done = bf16[1600,128]{1,0:T(8,128)(2,1)} async-done(((bf16[25600,128]{1,0:T(8,128)(2,1)}), bf16[1600,128]{1,0:T(8,128)(2,1)}) %reduce-scatter.2.cloned.1.call-update) | async-done | bytes 409616 | tf_op jit(solution)/shard_map/reduce_scatter | solution.py:27
  120.7 1.1 multiply_reduce_fusion.1
  122.0 1.1 slice_convert_fusion
  123.8 0.6 broadcast_in_dim.3
  124.4 4.0 %all-to-all-start = ((f32[4,1,320]{2,1,0:T(1,128)}), f32[4,1,320]{2,1,0:T(1,128)S(1)}, u32[]{:S(2)}, u32[]{:S(2)}) async-start(f32[4,1,320]{2,1,0:T(1,128)} %broadcast_in_dim.3), calls=%async_computation.1 | async-start | bytes 12288 | tf_op jit(solution)/shard_map/all_to_all | solution.py:41
  128.4 0.6 convert_bitcast_fusion.1
  129.5 3.0 %all-to-all-done = f32[4,1,320]{2,1,0:T(1,128)S(1)} async-done(((f32[4,1,320]{2,1,0:T(1,128)}), f32[4,1,320]{2,1,0:T(1,128)S(1)}, u32[]{:S(2)}, u32[]{:S(2)}) %all-to-all-start) | async-done | bytes 5152 | tf_op jit(solution)/shard_map/all_to_all | solution.py:41
  132.7 0.9 convert_bitcast_fusion
  133.5 0.9 fusion
  134.4 0.8 concatenate.11
  135.3 50.2 %all-gather.2.cloned.1.call-done = bf16[1280,2562]{1,0:T(8,128)(2,1)} async-done(((bf16[80,2562]{1,0:T(8,128)(2,1)}), bf16[1280,2562]{1,0:T(8,128)(2,1)}) %all-gather.2.cloned.1.call-update) | async-done | bytes 6558736 | tf_op jit(solution)/shard_map/all_gather | solution.py:61
  185.5 5.1 %slice_bitcast_fusion = (bf16[1280,1280]{0,1:T(8,128)(2,1)S(1)}, bf16[1280,1280]{1,0:T(8,128)(2,1)}) fusion(bf16[1280,2562]{1,0:T(8,128)(2,1)} %all-gather.2.cloned.1.call-done), kind=kLoop, calls=%fused_computation.1 | loop fusion | bytes 13107200 | tf_op jit(solution)/shard_map/transpose | solution.py:65
  190.5 3.4 %copy.44 = bf16[1280,1280]{1,0:T(8,128)(2,1)} copy(bf16[1280,1280]{0,1:T(8,128)(2,1)S(1)} %get-tuple-element.62) | data formatting | bytes 6553600
  193.9 2.0 %slice_reduce_fusion = (bf16[1280]{0:T(1024)(128)(2,1)}, bf16[1280]{0:T(1024)(128)(2,1)}) fusion(bf16[1280,2562]{1,0:T(8,128)(2,1)} %all-gather.2.cloned.1.call-done), kind=kLoop, calls=%fused_computation.8 | loop fusion | bytes 10240 | tf_op jit(solution)/shard_map/split | solution.py:62
  (29 shorter events, 1.8 us)
Async XLA Ops:
  7.2 113.6 %reduce-scatter.2.cloned.1.call-start = ((), (), s32[]{:S(2)}) async-start(), calls=%async_computation.2 | async-start | bytes 6963200 | tf_op jit(solution)/shard_map/reduce_scatter | solution.py:27
  51.9 0.7 copy-start.2
  51.9 0.7 copy-start.3
  51.9 38.1 %copy-start.1 = (f32[80,1280]{1,0:T(8,128)S(1)}, f32[80,1280]{1,0:T(8,128)}, u32[]{:S(2)}) copy-start(f32[80,1280]{1,0:T(8,128)} %param.12) | copy-start | bytes 1228804
  51.9 38.2 %copy-start = (f32[1280,80]{0,1:T(8,128)S(1)}, f32[1280,80]{0,1:T(8,128)}, u32[]{:S(2)}) copy-start(f32[1280,80]{0,1:T(8,128)} %param.13) | copy-start | bytes 1228804
  51.9 38.3 %copy-start.4 = (f32[80]{0:T(128)S(1)}, f32[80]{0:T(128)}, u32[]{:S(2)}) copy-start(f32[80]{0:T(128)} %param.14) | copy-start | bytes 964
  51.9 76.5 %copy-start.5 = (f32[80]{0:T(128)S(1)}, f32[80]{0:T(128)}, u32[]{:S(2)}) copy-start(f32[80]{0:T(128)} %param.15) | copy-start | bytes 964
  124.4 8.2 %all-to-all-start = ((f32[4,1,320]{2,1,0:T(1,128)}), f32[4,1,320]{2,1,0:T(1,128)S(1)}, u32[]{:S(2)}, u32[]{:S(2)}) async-start(f32[4,1,320]{2,1,0:T(1,128)} %broadcast_in_dim.3), calls=%async_computation.1 | async-start | bytes 12288 | tf_op jit(solution)/shard_map/all_to_all | solution.py:41
  128.4 57.1 %all-gather.2.cloned.1.call-start = ((), (), s32[]{:S(2)}) async-start(), calls=%async_computation.3 | async-start | bytes 7311360 | tf_op jit(solution)/shard_map/all_gather | solution.py:61
Sparse Core Ops, SparseCore 0:
  52.1 68.5 reduce-scatter.1
  135.4 50.0 all-gather.1
where the time goes:
time: 203 us
  waiting for transfers between devices  83.1 us (41%)
  local copies, waits for them, and re-layouts  49.6 us (24%)
  blocking collectives  37.4 us (18%)
  other arithmetic  14.5 us (7%)
  between operations  14.1 us (7%)
  starting transfers between devices  4.06 us (2%)
    all_gather x1, waiting for transfers between devices, rows_first(): out = lax.all_gather(both, axis, axis=0, tiled=True)  50.2 us
    psum x2, blocking collectives, one_axis_at_a_time(): return functools.reduce(lax.psum, axes, array)  37.4 us
    reduce_scatter x1, waiting for transfers between devices, sum_packed(): lax.psum_scatter(lines, axis, tiled=True).reshape(-1)  29.8 us
    reshape x1, local copies, waits for them, and re-layouts, sum_packed(): lines = jnp.concatenate([b.reshape(devices, -1) for b in parts], axis=1)  13.6 us
    unnamed x14, local copies, waits for them, and re-layouts  9.69 us
    concatenate x1, other arithmetic, sum_packed(): lines = jnp.concatenate([b.reshape(devices, -1) for b in parts], axis=1)  8.61 us
    transpose x1, local copies, waits for them, and re-layouts, split_up(): return jnp.moveaxis(array.reshape(*before, devices, -1, *after), dim, 0)  7.28 us
    reshape x1, local copies, waits for them, and re-layouts, sum_packed(): jnp.pad(lines, ((0, 0), (0, rows * 128 - lines.shape[1]))).reshape(-1, 128)  6.61 us
  transfers between devices with their start and end apart: 3, of which 3 were waited for; matrix products, arithmetic and copies ran while one was open for 1% of the time, Pallas kernels for 0%

commit v1 on v0

v1 whole, which is shorter than its diff:
```python
import functools

import jax
import jax.numpy as jnp
from jax import lax
from jax.experimental import pallas as pl
from jax.experimental.pallas import tpu as pltpu
from jax.sharding import Mesh
from jax.sharding import PartitionSpec as P

AXES = ("ens", "z", "core", "cols")
RATE = 0.4
LANES = 128
F32 = jnp.float32
BF16 = jnp.bfloat16


def cut(rows):
    parts, at = [], 0
    for size in (32, 32, 16):
        if at < rows:
            parts.append((at, min(size, rows - at)))
            at += size
    return parts


def kernel(
    dims,
    gu, gd, gn, gb, wu, wd, wn, wb,
    cu, cd, cn, cb, nu, nd, nn, nb,
    raw, g_u, g_d, pair_u, pair_d, rcv_u, rcv_d, w_u, w_d, fin_u, fin_d, full_d,
    slope, own, vin, vw, vplace, vown, vpair, vslot, vfull, sems,
):
    ring, cols, rows, wide = dims
    z, core, y = lax.axis_index("z"), lax.axis_index("core"), lax.axis_index("cols")
    other = 1 - core
    far, near = ring // 2, ring - 1 - ring // 2
    mean_rate = (ring * 2) ** -0.5
    place = z * 2 + core
    count = [0]
    sent = []

    def new_sem():
        count[0] += 1
        return sems.at[count[0] - 1]

    def at_z(shift):
        return lax.rem(z + (shift + ring), ring)

    def fetch(src, dst):
        copy = pltpu.make_async_copy(src, dst, new_sem())
        copy.start()
        return copy

    def send(src, dst, **where):
        copy = pltpu.make_async_remote_copy(
            src_ref=src, dst_ref=dst, send_sem=new_sem(), recv_sem=new_sem(),
            device_id=where, device_id_type=pl.DeviceIdType.MESH,
        )
        copy.start()
        sent.append(copy)
        return copy

    def block(zd, part, r0, n):
        return pl.ds(pl.multiple_of((zd * 2 + part) * rows + r0, 16), n)

    shifts = [far]
    for d in range(near, 0, -1):
        shifts += [d, -d]
    shifts.append(0)
    slot_of = {s: k for k, s in enumerate(shifts)}
    slot_of[-far] = slot_of[far]

    loads_mine, loads_other = [], []
    for s in shifts:
        zd = at_z(s)
        for part, out in ((other, loads_other), (core, loads_mine)):
            here = block(zd, part, 0, rows)
            out.append(fetch(gu.at[here], g_u.at[here]))
    small = [
        fetch(gn, vin.at[0]), fetch(gb, vin.at[1]), fetch(wn, vw.at[0]), fetch(wb, vw.at[1]),
    ]
    load_raw = fetch(gd, raw)
    load_w = [fetch(wu, w_u), fetch(wd, w_d)]

    barrier = pltpu.get_barrier_semaphore()
    peers = [{"core": other}, {"z": at_z(1)}, {"z": at_z(-1)}]
    others_y = [lax.rem(y + k, cols) for k in range(1, cols)]
    peers += [{"cols": o} for o in others_y]
    for peer in peers:
        pl.semaphore_signal(barrier, inc=1, device_id=peer, device_id_type=pl.DeviceIdType.MESH)
    pl.semaphore_wait(barrier, len(peers))

    mats = {
        "u": dict(g=g_u, pair=pair_u, rcv=rcv_u, w=w_u, fin=fin_u, full=cu, new=nu, k=0),
        "d": dict(g=g_d, pair=pair_d, rcv=rcv_d, w=w_d, fin=fin_d, full=full_d, new=nd, k=1),
    }

    def swap(name):
        m = mats[name]
        m["swaps"] = []
        for k, s in enumerate(shifts):
            if name == "u":
                loads_other[k].wait()
            zd = at_z(s)
            m["swaps"].append(
                send(m["g"].at[block(zd, other, 0, rows)], m["pair"].at[zd], core=other)
            )
        m["ready"] = set()

    def pair_sum(m, shift, r0, n):
        k = slot_of[shift]
        if k not in m["ready"]:
            if m is mats["u"]:
                loads_mine[k].wait()
            m["swaps"][k].wait_recv()
            m["ready"].add(k)
        zd = at_z(shift)
        mine = m["g"][block(zd, core, r0, n), :].astype(F32)
        return mine + m["pair"][zd, pl.ds(r0, n), :].astype(F32)

    flows = []
    for name, flip in (("u", 0), ("d", 1)):
        for i, (r0, n) in enumerate(cut(rows)):
            reach = (near, far) if (i + flip) % 2 == 0 else (far, near)
            flows.append(dict(m=name, r0=r0, n=n, reach=reach, rs={}, ag={}, to={}))

    def of(name):
        return [f for f in flows if f["m"] == name]

    def scatter(name, step):
        m = mats[name]
        for f in of(name):
            r0, n = f["r0"], f["n"]
            for d, sign in ((1, -1), (0, 1)):
                reach = f["reach"][d]
                if step > reach:
                    continue
                shift = sign * (reach - step + 1)
                if abs(shift) == far:
                    shift = far
                total = pair_sum(m, shift, r0, n)
                if step > 1:
                    f["rs"][d, step - 1].wait_recv()
                    total += m["rcv"][d, step - 2, pl.ds(r0, n), :].astype(F32)
                zd = at_z(shift)
                m["pair"][zd, pl.ds(r0, n), :] = total.astype(BF16)
                f["rs"][d, step] = send(
                    m["pair"].at[zd, pl.ds(r0, n)],
                    m["rcv"].at[d, step - 1, pl.ds(r0, n)],
                    z=at_z(sign),
                )

    def folded(x):
        out = x[:, :LANES]
        for j in range(1, x.shape[1] // LANES):
            out += x[:, j * LANES : (j + 1) * LANES]
        return out

    def share_with_cols(table, k, r0, n):
        return [
            send(table.at[k, y, pl.ds(r0, n)], table.at[k, y, pl.ds(r0, n)], cols=o)
            for o in others_y
        ]

    def finish_sum(name):
        m = mats[name]
        for f in of(name):
            r0, n = f["r0"], f["n"]
            total = pair_sum(m, 0, r0, n)
            for d in (1, 0):
                reach = f["reach"][d]
                f["rs"][d, reach].wait_recv()
                total += m["rcv"][d, reach - 1, pl.ds(r0, n), :].astype(F32)
            mean = total * mean_rate
            m["fin"][pl.ds(r0, n), :] = mean
            slope[m["k"], y, pl.ds(r0, n), :] = folded(mean * mean)
            f["sizes"] = share_with_cols(slope, m["k"], r0, n)

    def size_of(table, k, r0, n):
        total = table[k, 0, pl.ds(r0, n), :]
        for j in range(1, cols):
            total += table[k, j, pl.ds(r0, n), :]
        return jnp.sum(total, axis=1, keepdims=True)

    def update(name):
        m = mats[name]
        for c in m.pop("own_sizes"):
            c.wait_recv()
        for f in of(name):
            r0, n = f["r0"], f["n"]
            for c in f["sizes"]:
                c.wait_recv()
            ratio = jnp.sqrt(size_of(own, m["k"], r0, n)) * lax.rsqrt(
                size_of(slope, m["k"], r0, n) + 1e-06
            )
            new = m["w"][pl.ds(r0, n), :] - RATE * (m["fin"][pl.ds(r0, n), :] * ratio)
            m["new"][pl.ds(r0, n), :] = new
            here = m["full"].at[block(z, core, r0, n)]
            here[...] = new.astype(BF16)
            for d, sign in ((1, -1), (0, 1)):
                f["ag"][d, 1] = send(here, here, z=at_z(sign))
            f["to"][0, 0] = send(here, here, core=other)

    def pass_on(name, step):
        m = mats[name]
        for f in of(name):
            for d, sign in ((1, -1), (0, 1)):
                reach = f["reach"][d]
                if step > reach:
                    continue
                f["ag"][d, step].wait_recv()
                here = m["full"].at[block(at_z(-sign * step), core, f["r0"], f["n"])]
                if step < reach:
                    f["ag"][d, step + 1] = send(here, here, z=at_z(sign))
                f["to"][d, step] = send(here, here, core=other)

    def all_here(name):
        for f in of(name):
            for copy in f["to"].values():
                copy.wait_recv()

    def vectors_out():
        for copy in small:
            copy.wait()
        vplace[...] = jnp.zeros_like(vplace)
        for v in range(2):
            vplace[pl.ds(v, 1), pl.ds(0, rows)] = vw[v]
        placed = pltpu.roll(vplace[...], place * rows, 1)
        for v in range(2):
            vown[v] = placed[v : v + 1, :] - (RATE * mean_rate) * vin[v].astype(F32)
        return send(vown.at[other], vpair, core=other)

    vec = {}

    def vectors_ring(step):
        if step == 1:
            vec["swap"].wait_recv()
            vslot[z] = vown[core] + vpair[...]
        for d, sign in ((1, -1), (0, 1)):
            reach = (near, far)[d]
            if step > 1 and step - 1 <= reach:
                vec[d, step - 1].wait_recv()
            if step <= reach:
                here = vslot.at[at_z(-sign * (step - 1))]
                vec[d, step] = send(here, here, z=at_z(sign))

    def vectors_sum():
        total = vslot[0]
        for k in range(1, ring):
            total += vslot[k]
        vfull[core] = total
        vec["full"] = send(vfull.at[core], vfull.at[core], core=other)

    def vectors_in():
        vec["full"].wait_recv()
        back = lax.rem(ring * 2 - place, ring * 2) * rows
        for v, (c_ref, n_ref) in enumerate(((cn, nn), (cb, nb))):
            c_ref[...] = vfull[v].astype(BF16)
            vplace[pl.ds(v, 1), :] = vfull[v]
        turned = pltpu.roll(vplace[...], back, 1)
        for v, n_ref in enumerate((nn, nb)):
            n_ref[...] = turned[v : v + 1, :rows]

    def turn_in():
        load_raw.wait()

        def slab(j, _):
            here = pl.ds(pl.multiple_of(j * LANES, LANES), LANES)
            g_d[here, :] = raw[:, here].T
            return 0

        lax.fori_loop(0, ring * 2 * rows // LANES, slab, 0)

    def turn_out():
        def slab(j, _):
            here = pl.ds(pl.multiple_of(j * LANES, LANES), LANES)
            cd[:, here] = full_d[here, :].T
            return 0

        lax.fori_loop(0, ring * 2 * rows // LANES, slab, 0)

    def own_sizes():
        for copy in load_w:
            copy.wait()
        for name in ("u", "d"):
            m = mats[name]
            w = m["w"][...]
            own[m["k"], y] = folded(w * w)
            m["own_sizes"] = share_with_cols(own, m["k"], 0, rows)

    swap("u")
    scatter("u", 1)
    vec["swap"] = vectors_out()
    turn_in()
    swap("d")
    vectors_ring(1)
    own_sizes()
    steps = far
    for s in range(2, steps):
        scatter("u", s)
        vectors_ring(s)
    scatter("d", 1)
    if steps > 1:
        scatter("u", steps)
        vectors_ring(steps)
    if steps > 1:
        scatter("d", 2)
    finish_sum("u")
    for s in range(3, steps + 1):
        scatter("d", s)
    vectors_ring(steps + 1)
    vectors_sum()
    update("u")
    finish_sum("d")
    vectors_in()
    pass_on("u", 1)
    update("d")
    pass_on("d", 1)
    for s in range(2, steps):
        pass_on("u", s)
        pass_on("d", s)
    if steps > 1:
        pass_on("d", steps)
        pass_on("u", steps)
    all_here("d")
    turn_out()
    all_here("u")
    for copy in sent:
        copy.wait_send()


def per_device(ring, cols, grad_up, grad_down, grad_norm, grad_bias, *weights):
    weight_up, weight_down, weight_norm, weight_bias = weights
    rows, wide = weight_up.shape
    total = ring * 2 * rows
    any_spec = pl.BlockSpec(memory_space=pl.ANY)
    vmem = pl.BlockSpec(memory_space=pltpu.VMEM)
    shape = jax.ShapeDtypeStruct
    outs = (
        shape((total, wide), BF16), shape((wide, total), BF16),
        shape((1, total), BF16), shape((1, total), BF16),
        shape((rows, wide), F32), shape((rows, wide), F32),
        shape((1, rows), F32), shape((1, rows), F32),
    )
    far = ring // 2
    scratch = [
        pltpu.VMEM((wide, total), BF16),
        pltpu.VMEM((total, wide), BF16), pltpu.VMEM((total, wide), BF16),
        pltpu.VMEM((ring, rows, wide), BF16), pltpu.VMEM((ring, rows, wide), BF16),
        pltpu.VMEM((2, far, rows, wide), BF16), pltpu.VMEM((2, far, rows, wide), BF16),
        pltpu.VMEM((rows, wide), F32), pltpu.VMEM((rows, wide), F32),
        pltpu.VMEM((rows, wide), F32), pltpu.VMEM((rows, wide), F32),
        pltpu.VMEM((total, wide), BF16),
        pltpu.VMEM((2, cols, rows, LANES), F32), pltpu.VMEM((2, cols, rows, LANES), F32),
        pltpu.VMEM((2, 1, total), BF16), pltpu.VMEM((2, 1, rows), F32),
        pltpu.VMEM((8, total), F32), pltpu.VMEM((2, 1, total), F32),
        pltpu.VMEM((1, total), F32), pltpu.VMEM((ring, 1, total), F32),
        pltpu.VMEM((2, 1, total), F32),
        pltpu.SemaphoreType.DMA((448,)),
    ]
    got = pl.pallas_call(
        functools.partial(kernel, (ring, cols, rows, wide)),
        out_shape=outs,
        in_specs=[any_spec] * 8,
        out_specs=[vmem] * 8,
        scratch_shapes=scratch,
        compiler_params=pltpu.CompilerParams(
            collective_id=0, has_side_effects=True, vmem_limit_bytes=60 * 2**20
        ),
        name="step",
    )(
        grad_up[0], grad_down[0], grad_norm, grad_bias,
        weight_up, weight_down.T, weight_norm[None], weight_bias[None],
    )
    copy_up, copy_down, copy_norm, copy_bias, new_up, new_down, new_norm, new_bias = got
    return (
        copy_up, copy_down, copy_norm[0], copy_bias[0],
        new_up, new_down.T, new_norm[0], new_bias[0],
    )


def solution(mesh):
    ring, cols = mesh.shape["batch"] // 2, mesh.shape["cols"]
    finer = Mesh(mesh.devices.reshape(mesh.shape["ens"], ring, 2, cols), AXES)
    batch = ("z", "core")
    all_of = ("ens", "z", "core")
    placed = (
        P(all_of, None, "cols"), P(all_of, "cols", None), P(all_of, None), P(all_of, None),
        P(all_of, "cols"), P(("ens", "cols"), batch), P(all_of), P(all_of),
    )
    return jax.shard_map(
        functools.partial(per_device, ring, cols),
        mesh=finer,
        in_specs=placed,
        out_specs=(
            P("ens", "cols"), P(("ens", "cols"), None), P("ens"), P("ens"),
            P(all_of, "cols"), P(("ens", "cols"), batch), P(all_of), P(all_of),
        ),
        check_vma=False,
    )
```

time: 203 us -> 96.8 us (0.48)
  Pallas kernels: 0 us -> 85.1 us
  waiting for transfers between devices: 83.1 us -> 0 us
  local copies, waits for them, and re-layouts: 49.6 us -> 8.25 us
  blocking collectives: 37.4 us -> 0 us
  between operations: 14.1 us -> 0.66 us
  other arithmetic: 14.5 us -> 2.62 us
  starting transfers between devices: 4.06 us -> 0 us
    pallas_call x0 -> x1, Pallas kernels: none -> 85.1 us  [per_device(): pl.pallas_call(functools.partial(kernel, (ring, cols, rows, wide)), out_s...]
    all_gather x1 -> x0, waiting for transfers between devices: 50.2 us -> none  [rows_first(): out = lax.all_gather(both, axis, axis=0, tiled=True)]
    psum x2 -> x0, blocking collectives: 37.4 us -> none  [one_axis_at_a_time(): return functools.reduce(lax.psum, axes, array)]
    reduce_scatter x1 -> x0, waiting for transfers between devices: 29.8 us -> none  [sum_packed(): lax.psum_scatter(lines, axis, tiled=True).reshape(-1)]
    reshape x4 -> x0, local copies, waits for them, and re-layouts: 20.4 us -> none  [the longest x1 13.6 us: sum_packed(): lines = jnp.concatenate([b.reshape(devices, -1) for b in parts], axis=1)]
    transpose x2 -> x0, local copies, waits for them, and re-layouts: 12.3 us -> none  [the longest x1 7.28 us: split_up(): return jnp.moveaxis(array.reshape(*before, devices, -1, *after), dim, 0)]
    concatenate x2 -> x0, other arithmetic: 8.69 us -> none  [the longest x1 8.61 us: sum_packed(): lines = jnp.concatenate([b.reshape(devices, -1) for b in parts], axis=1)]
    all_to_all x1 -> x0, starting transfers between devices: 4.02 us -> none  [copy_for_each(): return lax.all_to_all(copies, axis, split_axis=0, concat_axis=0, tiled=True)]
  transfers between devices with their start and end apart: 3 -> 0, of which waited for: 3 -> 0; matrix products, arithmetic and copies ran while one was open for 1% -> 0% of each run, Pallas kernels for 0% -> 0%
where the time goes in v1:
time: 96.8 us; the launch traced here: 96.7 us
  Pallas kernels  85.1 us (88%)
  local copies, waits for them, and re-layouts  8.25 us (9%)
  other arithmetic  2.62 us (3%)
    pallas_call x1, Pallas kernels, per_device(): pl.pallas_call(functools.partial(kernel, (ring, cols, rows, wide)), out_s...  85.1 us
    unnamed x16, local copies, waits for them, and re-layouts  8.25 us
    pallas_call x2, other arithmetic, per_device(): pl.pallas_call(functools.partial(kernel, (ring, cols, rows, wide)), out_s...  2.62 us

profile of v1, /device:TPU:1, one launch (start us, length us, event | category | flops | bytes accessed | tf_op | source)
XLA Modules:
  0.0 96.7 jit_solution(14459876419086779173)
XLA Ops:
  0.6 85.1 %step.1 = (bf16[1280,1280]{1,0:T(8,128)(2,1)}, bf16[1280,1280]{1,0:T(8,128)(2,1)}, bf16[1,1280]{1,0:T(2,128)(2,1)}, bf16[1,1280]{1,0:T(2,128)(2,1)}, f32[80,1280...) custom-call(bf16[1280,1280]{1,0:T(8,128)(2,1)} %bitcast.8, bf16[1280,1280]{1,0:T(8,128)(2,1)} %bitcast.9, ...), custom_call_target="tpu_custom_call" | custom-call | tf_op jit(solution)/shard_map/step/pallas_call | solution.py:362
  85.8 1.3 %reduce = bf16[1280]{0:T(1024)(128)(2,1)} reduce(bf16[1,1280]{1,0:T(2,128)(2,1)} %get-tuple-element.18, bf16[]{:T(256)} %constant.7), dimensions={0}, to_apply=%get-tuple-element.18.reduce_sub_computation | reduce | bytes 5122 | tf_op jit(solution)/shard_map/step/pallas_call | solution.py:362
  87.1 1.3 %reduce.1 = bf16[1280]{0:T(1024)(128)(2,1)} reduce(bf16[1,1280]{1,0:T(2,128)(2,1)} %get-tuple-element.19, bf16[]{:T(256)} %constant.7), dimensions={0}, to_apply=%get-tuple-element.19.reduce_sub_computation | reduce | bytes 5122 | tf_op jit(solution)/shard_map/step/pallas_call | solution.py:362
  88.4 0.0 copy-start
  88.4 4.0 %copy.22 = bf16[1280,1280]{1,0:T(8,128)(2,1)} copy(bf16[1280,1280]{1,0:T(8,128)(2,1)} %get-tuple-element.32) | data formatting | bytes 6553600
  92.4 0.0 copy-done
  92.4 0.0 copy-start.2
  92.4 0.0 copy-start.1
  92.4 0.0 copy-start.4
  92.4 0.0 copy-start.3
  92.4 1.7 %copy.23 = bf16[1280,1280]{1,0:T(8,128)(2,1)} copy(bf16[1280,1280]{1,0:T(8,128)(2,1)S(1)} %copy-done) | data formatting | bytes 6553600
  94.1 0.0 copy-done.2
  94.1 0.8 copy.24
  94.9 0.0 copy-done.1
  94.9 0.8 copy.25
  95.6 0.0 copy-done.4
  95.6 0.5 copy.26
  96.1 0.0 copy-done.3
  96.1 0.5 copy.27
Async XLA Ops:
  88.4 4.0 %copy-start = (bf16[1280,1280]{1,0:T(8,128)(2,1)S(1)}, bf16[1280,1280]{1,0:T(8,128)(2,1)}, u32[]{:S(2)}) copy-start(bf16[1280,1280]{1,0:T(8,128)(2,1)} %get-tuple-element.33) | copy-start | bytes 9830404
  92.4 1.7 %copy-start.2 = (f32[80,1280]{1,0:T(8,128)S(1)}, f32[80,1280]{1,0:T(8,128)}, u32[]{:S(2)}) copy-start(f32[80,1280]{1,0:T(8,128)} %get-tuple-element.36) | copy-start | bytes 1228804
  92.4 2.5 %copy-start.1 = (f32[80,1280]{1,0:T(8,128)S(1)}, f32[80,1280]{1,0:T(8,128)}, u32[]{:S(2)}) copy-start(f32[80,1280]{1,0:T(8,128)} %get-tuple-element.21) | copy-start | bytes 1228804
  92.4 3.2 %copy-start.4 = (f32[1,80]{1,0:T(1,128)S(1)}, f32[1,80]{1,0:T(1,128)}, u32[]{:S(2)}) copy-start(f32[1,80]{1,0:T(1,128)} %get-tuple-element.22) | copy-start | bytes 964
  92.4 3.7 %copy-start.3 = (f32[1,80]{1,0:T(1,128)S(1)}, f32[1,80]{1,0:T(1,128)}, u32[]{:S(2)}) copy-start(f32[1,80]{1,0:T(1,128)} %get-tuple-element.23) | copy-start | bytes 964

commit v2 on v1

--- a/solution.py
+++ b/solution.py
@@ -10,6 +10,7 @@
 
 AXES = ("ens", "z", "core", "cols")
 RATE = 0.4
+VL = 52
 LANES = 128
 F32 = jnp.float32
 BF16 = jnp.bfloat16
@@ -27,8 +28,8 @@
 def kernel(
     dims,
     gu, gd, gn, gb, wu, wd, wn, wb,
-    cu, cd, cn, cb, nu, nd, nn, nb,
-    raw, g_u, g_d, pair_u, pair_d, rcv_u, rcv_d, w_u, w_d, fin_u, fin_d, full_d,
+    cu, full_d, cn, cb, nu, nd, nn, nb,
+    raw, g_u, g_d, pair_u, pair_d, rcv_u, rcv_d, w_u, w_d, fin_u, fin_d,
     slope, own, vin, vw, vplace, vown, vpair, vslot, vfull, sems,
 ):
     ring, cols, rows, wide = dims
@@ -80,8 +81,6 @@
     small = [
         fetch(gn, vin.at[0]), fetch(gb, vin.at[1]), fetch(wn, vw.at[0]), fetch(wb, vw.at[1]),
     ]
-    load_raw = fetch(gd, raw)
-    load_w = [fetch(wu, w_u), fetch(wd, w_d)]
 
     barrier = pltpu.get_barrier_semaphore()
     peers = [{"core": other}, {"z": at_z(1)}, {"z": at_z(-1)}]
@@ -272,14 +271,6 @@
 
         lax.fori_loop(0, ring * 2 * rows // LANES, slab, 0)
 
-    def turn_out():
-        def slab(j, _):
-            here = pl.ds(pl.multiple_of(j * LANES, LANES), LANES)
-            cd[:, here] = full_d[here, :].T
-            return 0
-
-        lax.fori_loop(0, ring * 2 * rows // LANES, slab, 0)
-
     def own_sizes():
         for copy in load_w:
             copy.wait()
@@ -290,13 +281,15 @@
             m["own_sizes"] = share_with_cols(own, m["k"], 0, rows)
 
     swap("u")
+    load_raw = fetch(gd, raw)
+    load_w = [fetch(wu, w_u), fetch(wd, w_d)]
+    steps = far
     scatter("u", 1)
     vec["swap"] = vectors_out()
     turn_in()
     swap("d")
     vectors_ring(1)
     own_sizes()
-    steps = far
     for s in range(2, steps):
         scatter("u", s)
         vectors_ring(s)
@@ -304,7 +297,6 @@
     if steps > 1:
         scatter("u", steps)
         vectors_ring(steps)
-    if steps > 1:
         scatter("d", 2)
     finish_sum("u")
     for s in range(3, steps + 1):
@@ -313,21 +305,39 @@
     vectors_sum()
     update("u")
     finish_sum("d")
-    vectors_in()
     pass_on("u", 1)
     update("d")
-    pass_on("d", 1)
-    for s in range(2, steps):
+    vectors_in()
+    for s in range(2, steps + 1):
         pass_on("u", s)
-        pass_on("d", s)
-    if steps > 1:
-        pass_on("d", steps)
-        pass_on("u", steps)
+        pass_on("d", s - 1)
+    pass_on("d", steps)
     all_here("d")
-    turn_out()
     all_here("u")
     for copy in sent:
         copy.wait_send()
+
+
+def put(cu, full_d, cn, cb, nu, nd, nn, nb, cu_o, cd_o, cn_o, cb_o, nu_o, nd_o, nn_o, nb_o, turned, sems):
+    copies = []
+
+    def write(src, dst):
+        copies.append(pltpu.make_async_copy(src, dst, sems.at[len(copies)]))
+        copies[-1].start()
+
+    wide = turned.shape[0]
+    for r in range(0, wide, LANES):
+        here = pl.ds(r, LANES)
+        turned[here, :] = full_d[:, here].T
+        write(turned.at[here], cd_o.at[here])
+        part = pl.ds(r * cu.shape[0] // wide, LANES * cu.shape[0] // wide)
+        write(cu.at[part], cu_o.at[part])
+    for src, dst in ((nu, nu_o), (nd, nd_o), (nn, nn_o), (nb, nb_o)):
+        write(src, dst)
+    cn_o[...] = cn[0, :]
+    cb_o[...] = cb[0, :]
+    for copy in copies:
+        copy.wait()
 
 
 def per_device(ring, cols, grad_up, grad_down, grad_norm, grad_bias, *weights):
@@ -351,7 +361,6 @@
         pltpu.VMEM((2, far, rows, wide), BF16), pltpu.VMEM((2, far, rows, wide), BF16),
         pltpu.VMEM((rows, wide), F32), pltpu.VMEM((rows, wide), F32),
         pltpu.VMEM((rows, wide), F32), pltpu.VMEM((rows, wide), F32),
-        pltpu.VMEM((total, wide), BF16),
         pltpu.VMEM((2, cols, rows, LANES), F32), pltpu.VMEM((2, cols, rows, LANES), F32),
         pltpu.VMEM((2, 1, total), BF16), pltpu.VMEM((2, 1, rows), F32),
         pltpu.VMEM((8, total), F32), pltpu.VMEM((2, 1, total), F32),
@@ -361,21 +370,41 @@
     ]
     got = pl.pallas_call(
         functools.partial(kernel, (ring, cols, rows, wide)),
-        out_shape=outs,
-        in_specs=[any_spec] * 8,
+        out_shape=[
+            pltpu.VMEM((total, wide) if k == 1 else o.shape, o.dtype) for k, o in enumerate(outs)
+        ],
+        in_specs=[pl.BlockSpec(memory_space=pltpu.HBM)] * 8,
         out_specs=[vmem] * 8,
         scratch_shapes=scratch,
         compiler_params=pltpu.CompilerParams(
-            collective_id=0, has_side_effects=True, vmem_limit_bytes=60 * 2**20
+            collective_id=0, has_side_effects=True, vmem_limit_bytes=VL * 2**20
         ),
         name="step",
     )(
-        grad_up[0], grad_down[0], grad_norm, grad_bias,
-        weight_up, weight_down.T, weight_norm[None], weight_bias[None],
+        *(
+            pltpu.with_memory_space_constraint(a, pltpu.HBM)
+            for a in (
+                grad_up[0], grad_down[0], grad_norm, grad_bias,
+                weight_up, weight_down.T, weight_norm[None], weight_bias[None],
+            )
+        )
     )
+    flat = shape((total,), BF16)
+    got = pl.pallas_call(
+        put,
+        out_shape=(*outs[:2], flat, flat, *outs[4:]),
+        in_specs=[vmem] * 8,
+        out_specs=[any_spec] * 2 + [vmem] * 2 + [any_spec] * 4,
+        scratch_shapes=[
+            pltpu.VMEM((wide, total), BF16),
+            pltpu.SemaphoreType.DMA((2 * wide // LANES + 4,)),
+        ],
+        compiler_params=pltpu.CompilerParams(vmem_limit_bytes=8 * 2**20),
+        name="put",
+    )(*got)
     copy_up, copy_down, copy_norm, copy_bias, new_up, new_down, new_norm, new_bias = got
     return (
-        copy_up, copy_down, copy_norm[0], copy_bias[0],
+        copy_up, copy_down, copy_norm, copy_bias,
         new_up, new_down.T, new_norm[0], new_bias[0],
     )
 

time: 96.8 us -> 86.5 us (0.89)
  local copies, waits for them, and re-layouts: 8.25 us -> 0 us
  other arithmetic: 2.62 us -> 0 us
    unnamed x16 -> x0, local copies, waits for them, and re-layouts: 8.25 us -> none
    pallas_call x0 -> x1, Pallas kernels: none -> 3.9 us  [per_device(): pl.pallas_call(put, out_shape=(*outs[:2], flat, flat, *outs[4:]), in_spec...]
    pallas_call x1, Pallas kernels: 85.1 us -> 81.9 us  [per_device(): pl.pallas_call(functools.partial(kernel, (ring, cols, rows, wide)), out_s...]
    pallas_call x2 -> x0, other arithmetic: 2.62 us -> none  [per_device(): pl.pallas_call(functools.partial(kernel, (ring, cols, rows, wide)), out_s...]
where the time goes in v2:
time: 86.5 us; the launch traced here: 86.4 us
  Pallas kernels  85.8 us (99%)
    pallas_call x1, Pallas kernels, per_device(): pl.pallas_call(functools.partial(kernel, (ring, cols, rows, wide)), out_s...  81.9 us
    pallas_call x1, Pallas kernels, per_device(): pl.pallas_call(put, out_shape=(*outs[:2], flat, flat, *outs[4:]), in_spec...  3.9 us

profile of v2, /device:TPU:1, one launch (start us, length us, event | category | flops | bytes accessed | tf_op | source)
XLA Modules:
  0.0 86.4 jit_solution(15470619301720925218)
XLA Ops:
  0.6 81.9 %step.1 = (bf16[1280,1280]{1,0:T(8,128)(2,1)S(1)}, bf16[1280,1280]{1,0:T(8,128)(2,1)S(1)}, bf16[1,1280]{1,0:T(2,128)(2,1)S(1)}, bf16[1,1280]{1,0:T(2,128)(2,1)S(...) custom-call(bf16[1280,1280]{1,0:T(8,128)(2,1)} %bitcast.8, ...), custom_call_target="tpu_custom_call" | custom-call | tf_op jit(solution)/shard_map/step/pallas_call | solution.py:371
  82.5 3.9 %put.1 = (bf16[1280,1280]{1,0:T(8,128)(2,1)}, bf16[1280,1280]{1,0:T(8,128)(2,1)}, bf16[1280]{0:T(1024)(128)(2,1)}, bf16[1280]{0:T(1024)(128)(2,1)}, f32[80,1280]...) custom-call(bf16[1280,1280]{1,0:T(8,128)(2,1)S(1)} %get-tuple-element.24.cu, ...), custom_call_target="tpu_custom_call" | custom-call | tf_op jit(solution)/shard_map/put/pallas_call | solution.py:393

commit v3 on v2

--- a/solution.py
+++ b/solution.py
@@ -30,7 +30,7 @@
     gu, gd, gn, gb, wu, wd, wn, wb,
     cu, full_d, cn, cb, nu, nd, nn, nb,
     raw, g_u, g_d, pair_u, pair_d, rcv_u, rcv_d, w_u, w_d, fin_u, fin_d,
-    slope, own, vin, vw, vplace, vown, vpair, vslot, vfull, sems,
+    slope, own, vin, vw, vplace, vown, vpair, vslot, vfull, sems, gates,
 ):
     ring, cols, rows, wide = dims
     z, core, y = lax.axis_index("z"), lax.axis_index("core"), lax.axis_index("cols")
@@ -73,50 +73,58 @@
     slot_of[-far] = slot_of[far]
 
     loads_mine, loads_other = [], []
-    for s in shifts:
-        zd = at_z(s)
-        for part, out in ((other, loads_other), (core, loads_mine)):
-            here = block(zd, part, 0, rows)
+    first = 3
+
+    def load(part, out, which):
+        for s in which:
+            here = block(at_z(s), part, 0, rows)
             out.append(fetch(gu.at[here], g_u.at[here]))
+
+    load(other, loads_other, shifts[:first])
+    load(core, loads_mine, shifts[:first])
+    load(other, loads_other, shifts[first:])
+    load(core, loads_mine, shifts[first:])
+    load_raw = fetch(gd, raw)
+    load_w = [fetch(wu, w_u), fetch(wd, w_d)]
     small = [
         fetch(gn, vin.at[0]), fetch(gb, vin.at[1]), fetch(wn, vw.at[0]), fetch(wb, vw.at[1]),
     ]
 
     barrier = pltpu.get_barrier_semaphore()
-    peers = [{"core": other}, {"z": at_z(1)}, {"z": at_z(-1)}]
     others_y = [lax.rem(y + k, cols) for k in range(1, cols)]
-    peers += [{"cols": o} for o in others_y]
-    for peer in peers:
-        pl.semaphore_signal(barrier, inc=1, device_id=peer, device_id_type=pl.DeviceIdType.MESH)
-    pl.semaphore_wait(barrier, len(peers))
+
+    def signal(sem, **where):
+        pl.semaphore_signal(sem, inc=1, device_id=where, device_id_type=pl.DeviceIdType.MESH)
+
+    for shift in (1, -1):
+        signal(barrier, z=at_z(shift), core=1)
+    for o in others_y:
+        signal(barrier, cols=o, core=0)
+
+    @pl.when(core == 0)
+    def _():
+        signal(barrier, core=1)
+        pl.semaphore_wait(gates.at[0], 1)
+
+    @pl.when(core == 1)
+    def _():
+        pl.semaphore_wait(barrier, 5)
+        signal(gates.at[0], core=0)
+
+    def meet_columns():
+        @pl.when(core == 0)
+        def _():
+            pl.semaphore_wait(barrier, 2 * len(others_y))
+            signal(gates.at[1], core=1)
+
+        @pl.when(core == 1)
+        def _():
+            pl.semaphore_wait(gates.at[1], 1)
 
     mats = {
-        "u": dict(g=g_u, pair=pair_u, rcv=rcv_u, w=w_u, fin=fin_u, full=cu, new=nu, k=0),
-        "d": dict(g=g_d, pair=pair_d, rcv=rcv_d, w=w_d, fin=fin_d, full=full_d, new=nd, k=1),
+        "u": dict(g=g_u, pair=pair_u, rcv=rcv_u, w=w_u, fin=fin_u, full=cu, new=nu, k=0, swaps={}, ready=set(), mine=set()),
+        "d": dict(g=g_d, pair=pair_d, rcv=rcv_d, w=w_d, fin=fin_d, full=full_d, new=nd, k=1, swaps={}, ready=set(), mine=set()),
     }
-
-    def swap(name):
-        m = mats[name]
-        m["swaps"] = []
-        for k, s in enumerate(shifts):
-            if name == "u":
-                loads_other[k].wait()
-            zd = at_z(s)
-            m["swaps"].append(
-                send(m["g"].at[block(zd, other, 0, rows)], m["pair"].at[zd], core=other)
-            )
-        m["ready"] = set()
-
-    def pair_sum(m, shift, r0, n):
-        k = slot_of[shift]
-        if k not in m["ready"]:
-            if m is mats["u"]:
-                loads_mine[k].wait()
-            m["swaps"][k].wait_recv()
-            m["ready"].add(k)
-        zd = at_z(shift)
-        mine = m["g"][block(zd, core, r0, n), :].astype(F32)
-        return mine + m["pair"][zd, pl.ds(r0, n), :].astype(F32)
 
     flows = []
     for name, flip in (("u", 0), ("d", 1)):
@@ -126,6 +134,44 @@
 
     def of(name):
         return [f for f in flows if f["m"] == name]
+
+    def swap(name, begin=0, end=None):
+        m = mats[name]
+        for k, s in list(enumerate(shifts))[begin:end]:
+            if name == "u":
+                loads_other[k].wait()
+            zd = at_z(s)
+            m["swaps"][k, 0] = send(
+                m["g"].at[block(zd, other, 0, rows)], m["pair"].at[zd], core=other
+            )
+
+    def swap_first(name):
+        m = mats[name]
+        for copy in loads_other[:first]:
+            copy.wait()
+        now, later = [], []
+        for f in of(name):
+            early = {far, f["reach"][0] if f["reach"][0] != far else -f["reach"][1]}
+            for k, s in enumerate(shifts[:first]):
+                (now if s in early else later).append((k, s, f["r0"], f["n"]))
+        for k, s, r0, n in now + later:
+            zd = at_z(s)
+            m["swaps"][k, r0] = send(
+                m["g"].at[block(zd, other, r0, n)], m["pair"].at[zd, pl.ds(r0, n)], core=other
+            )
+
+    def pair_sum(m, shift, r0, n):
+        k = slot_of[shift]
+        if m is mats["u"] and k not in m["mine"]:
+            loads_mine[k].wait()
+            m["mine"].add(k)
+        key = (k, r0) if (k, r0) in m["swaps"] else (k, 0)
+        if key not in m["ready"]:
+            m["swaps"][key].wait_recv()
+            m["ready"].add(key)
+        zd = at_z(shift)
+        mine = m["g"][block(zd, core, r0, n), :].astype(F32)
+        return mine + m["pair"][zd, pl.ds(r0, n), :].astype(F32)
 
     def scatter(name, step):
         m = mats[name]
@@ -280,45 +326,48 @@
             own[m["k"], y] = folded(w * w)
             m["own_sizes"] = share_with_cols(own, m["k"], 0, rows)
 
-    swap("u")
-    load_raw = fetch(gd, raw)
-    load_w = [fetch(wu, w_u), fetch(wd, w_d)]
+    swap_first("u")
     steps = far
     scatter("u", 1)
+    swap("u", first)
     vec["swap"] = vectors_out()
     turn_in()
     swap("d")
     vectors_ring(1)
+    meet_columns()
     own_sizes()
-    for s in range(2, steps):
-        scatter("u", s)
-        vectors_ring(s)
+    scatter("u", 2)
+    vectors_ring(2)
     scatter("d", 1)
-    if steps > 1:
-        scatter("u", steps)
-        vectors_ring(steps)
-        scatter("d", 2)
+    scatter("u", 3)
+    vectors_ring(3)
+    scatter("d", 2)
+    scatter("u", 4)
+    vectors_ring(4)
+    scatter("d", 3)
     finish_sum("u")
-    for s in range(3, steps + 1):
-        scatter("d", s)
-    vectors_ring(steps + 1)
+    scatter("d", 4)
+    vectors_ring(5)
     vectors_sum()
     update("u")
     finish_sum("d")
     pass_on("u", 1)
     update("d")
     vectors_in()
-    for s in range(2, steps + 1):
-        pass_on("u", s)
-        pass_on("d", s - 1)
-    pass_on("d", steps)
+    pass_on("u", 2)
+    pass_on("d", 1)
+    pass_on("d", 2)
+    pass_on("u", 3)
+    pass_on("d", 3)
+    pass_on("u", 4)
+    pass_on("d", 4)
     all_here("d")
     all_here("u")
     for copy in sent:
         copy.wait_send()
 
 
-def put(cu, full_d, cn, cb, nu, nd, nn, nb, cu_o, cd_o, cn_o, cb_o, nu_o, nd_o, nn_o, nb_o, turned, sems):
+def put(cu, full_d, cn, cb, nu, nd, nn, nb, cu_o, cd_o, cn_o, cb_o, nu_o, nd_o, nn_o, nb_o, turned, line_n, line_b, sems):
     copies = []
 
     def write(src, dst):
@@ -334,8 +383,9 @@
         write(cu.at[part], cu_o.at[part])
     for src, dst in ((nu, nu_o), (nd, nd_o), (nn, nn_o), (nb, nb_o)):
         write(src, dst)
-    cn_o[...] = cn[0, :]
-    cb_o[...] = cb[0, :]
+    for src, line, dst in ((cn, line_n, cn_o), (cb, line_b, cb_o)):
+        line[...] = src[0, :]
+        write(line, dst)
     for copy in copies:
         copy.wait()
 
@@ -366,7 +416,8 @@
         pltpu.VMEM((8, total), F32), pltpu.VMEM((2, 1, total), F32),
         pltpu.VMEM((1, total), F32), pltpu.VMEM((ring, 1, total), F32),
         pltpu.VMEM((2, 1, total), F32),
-        pltpu.SemaphoreType.DMA((448,)),
+        pltpu.SemaphoreType.DMA((480,)),
+        pltpu.SemaphoreType.REGULAR((2,)),
     ]
     got = pl.pallas_call(
         functools.partial(kernel, (ring, cols, rows, wide)),
@@ -394,10 +445,11 @@
         put,
         out_shape=(*outs[:2], flat, flat, *outs[4:]),
         in_specs=[vmem] * 8,
-        out_specs=[any_spec] * 2 + [vmem] * 2 + [any_spec] * 4,
+        out_specs=[any_spec] * 8,
         scratch_shapes=[
             pltpu.VMEM((wide, total), BF16),
-            pltpu.SemaphoreType.DMA((2 * wide // LANES + 4,)),
+            pltpu.VMEM((total,), BF16), pltpu.VMEM((total,), BF16),
+            pltpu.SemaphoreType.DMA((2 * wide // LANES + 6,)),
         ],
         compiler_params=pltpu.CompilerParams(vmem_limit_bytes=8 * 2**20),
         name="put",

time: 86.5 us -> 83.8 us (0.969)
  Pallas kernels: 85.8 us -> 83 us
    pallas_call x1, Pallas kernels: 81.9 us -> 79.7 us  [per_device(): pl.pallas_call(functools.partial(kernel, (ring, cols, rows, wide)), out_s...]
where the time goes in v3:
time: 83.8 us; the launch traced here: 83.7 us
  Pallas kernels  83 us (99%)
    pallas_call x1, Pallas kernels, per_device(): pl.pallas_call(functools.partial(kernel, (ring, cols, rows, wide)), out_s...  79.7 us
    pallas_call x1, Pallas kernels, per_device(): pl.pallas_call(put, out_shape=(*outs[:2], flat, flat, *outs[4:]), in_spec...  3.34 us

profile of v3, /device:TPU:1, one launch (start us, length us, event | category | flops | bytes accessed | tf_op | source)
XLA Modules:
  0.0 83.7 jit_solution(6596314246081813967)
XLA Ops:
  0.6 79.7 %step.1 = (bf16[1280,1280]{1,0:T(8,128)(2,1)S(1)}, bf16[1280,1280]{1,0:T(8,128)(2,1)S(1)}, bf16[1,1280]{1,0:T(2,128)(2,1)S(1)}, bf16[1,1280]{1,0:T(2,128)(2,1)S(...) custom-call(bf16[1280,1280]{1,0:T(8,128)(2,1)} %bitcast.8, ...), custom_call_target="tpu_custom_call" | custom-call | tf_op jit(solution)/shard_map/step/pallas_call | solution.py:422
  80.3 3.3 %put.1 = (bf16[1280,1280]{1,0:T(8,128)(2,1)}, bf16[1280,1280]{1,0:T(8,128)(2,1)}, bf16[1280]{0:T(1024)(128)(2,1)}, bf16[1280]{0:T(1024)(128)(2,1)}, f32[80,1280]...) custom-call(bf16[1280,1280]{1,0:T(8,128)(2,1)S(1)} %get-tuple-element.24.cu, ...), custom_call_target="tpu_custom_call" | custom-call | tf_op jit(solution)/shard_map/put/pallas_call | solution.py:444
